TPU v7x, 32 devices: a 4x4x1 block of a 4x4x8 slice. The times are simulated.
32 devices in a mesh: rep: 1 (over z), dp: 32 (over x, y, core).
Axes of the slice: x: 4, y: 4, z: 1, core: 2. Of those that a mesh axis runs over, the one named last changes fastest.
The devices are a block of a 4x4x8 slice.
Arguments:
- x: bfloat16 [32, 2048, 640], P(('rep', 'dp'))
- dy: bfloat16 [32, 2048, 640], P(('rep', 'dp'))
- w_gate: bfloat16 [2, 640, 3200], replicated
- w_up: bfloat16 [2, 640, 3200], replicated
- w_down: bfloat16 [2, 3200, 640], replicated
- m_w_gate: float32 [2, 640, 3200], replicated
- m_w_up: float32 [2, 640, 3200], replicated
- m_w_down: float32 [2, 3200, 640], replicated
- v_w_gate: float32 [2, 640, 3200], replicated
- v_w_up: float32 [2, 640, 3200], replicated
- v_w_down: float32 [2, 3200, 640], replicated
Outputs:
- output 1: bfloat16 [2, 640, 3200], P('rep')
- output 2: bfloat16 [2, 640, 3200], P('rep')
- output 3: bfloat16 [2, 3200, 640], P('rep')
- output 4: float32 [2, 640, 3200], P('rep')
- output 5: float32 [2, 640, 3200], P('rep')
- output 6: float32 [2, 3200, 640], P('rep')
- output 7: float32 [2, 640, 3200], P('rep')
- output 8: float32 [2, 640, 3200], P('rep')
- output 9: float32 [2, 3200, 640], P('rep')
All inputs are finite; a program needn't handle non-finite values.
Results may differ from a plain program's by a relative error of at most 0.022.
Values are sent between devices in bfloat16 or wider.
A program may use at most 768 MiB of HBM per device.

v0:
```python
import jax
import jax.numpy as jnp
from jax import lax
from jax.sharding import PartitionSpec as P

NAMES = ("w_gate", "w_up", "w_down")


def matmul(a, w):
    return jnp.dot(a, w, preferred_element_type=jnp.float32).astype(jnp.bfloat16)


def normed(h):
    wide = h.astype(jnp.float32)
    scale = lax.rsqrt(jnp.mean(wide**2, -1, keepdims=True) + 1e-6)
    return (wide * scale).astype(jnp.bfloat16)


def layer(h, w):
    a = normed(h)
    gate = jnp.dot(a, w["w_gate"], preferred_element_type=jnp.float32)
    up = jnp.dot(a, w["w_up"], preferred_element_type=jnp.float32)
    return h + matmul((jax.nn.silu(gate) * up).astype(jnp.bfloat16), w["w_down"])


def adamw(w, m, v, g):
    m = 0.9 * m + 0.1 * g
    v = 0.95 * v + 0.05 * g * g
    step = m * lax.rsqrt(v + 1e-8) + 0.1 * w
    return (w - 0.02 * step).astype(jnp.bfloat16), m, v


def solution(mesh):
    def step(x, dy, *arrays):
        weights, m, v = (arrays[i : i + 3] for i in (0, 3, 6))
        layers = weights[0].shape[0]
        h, kept = x[0], []
        for number in range(layers):
            kept.append(h)
            h = layer(h, {name: w[number] for name, w in zip(NAMES, weights, strict=True)})
        by_h, summed = dy[0], [None] * layers
        for number in reversed(range(layers)):
            _, back = jax.vjp(lambda w, h: layer(h, w), {name: w[number] for name, w in zip(NAMES, weights, strict=True)}, kept[number])
            by_w, by_h = back(by_h)
            summed[number] = [lax.psum(by_w[name], "dp") for name in NAMES]
        gradients = [jnp.stack([summed[number][i] for number in range(layers)]).astype(jnp.float32) for i in range(3)]
        new = [adamw(w.astype(jnp.float32), m, v, g) for w, m, v, g in zip(weights, m, v, gradients, strict=True)]
        return tuple(one[which] for which in range(3) for one in new)

    return jax.shard_map(
        step,
        mesh=mesh,
        in_specs=(P(("rep", "dp"), None, None),) * 2 + (P(None, None, None),) * 9,
        out_specs=(P("rep", None, None),) * 9,
        check_vma=False,
    )
```

profile of v0, /device:TPU:97, one launch (start us, length us, event | category | flops | bytes accessed | tf_op | source)
XLA Modules:
  0.0 594.4 jit_solution(16687875115392016940)
XLA Ops:
  7.2 0.1 all-reduce.3.cloned.1.call-start
  7.3 3.0 copy.20
  10.3 0.0 copy-start.1
  10.3 0.6 fusion.44
  10.9 4.7 copy.21
  15.6 16.4 %convolution_convert_fusion.1 = bf16[2048,3200]{1,0:T(8,128)(2,1)} fusion(bf16[2,3200,640]{2,1,0:T(8,128)(2,1)} %param.15, bf16[1,2048,640]{2,1,0:T(8,128)(2,1)} %param.12), kind=kOutput, calls=%fused_computation.50 | convolution fusion | flops 8395161600 | bytes 19824640 | tf_op jit(solution)/shard_map/transpose(jvp())/dot_general | solution.py:10
  32.0 16.7 %fusion.65 = f32[2048,3200]{1,0:T(8,128)} fusion(bf16[2,640,3200]{2,1,0:T(8,128)(2,1)} %param.13, bf16[1,2048,640]{2,1,0:T(8,128)(2,1)S(1)} %copy-done.7, f32[2048]{0:T(1024)S(1)} %add_rsqrt_fusion), kind=kOutput, calls=%fused_computation.96 | convolution fusion | flops 8392540160 | bytes 32940032 | tf_op jit(solution)/shard_map/dot_general | solution.py:21
  48.7 28.3 %multiply_convert_fusion.1 = (bf16[2048,3200]{1,0:T(8,128)(2,1)}, f32[2048,3200]{1,0:T(8,128)}) fusion(f32[2048,3200]{1,0:T(8,128)} %fusion.65, bf16[2,640,3200]{2,1,0:T(8,128)(2,1)} %param.14, bf16[1,2048,640]{2,1,0:T(8,128)(2,1)} %param.11, f32[2048]{0:T(1024)S(1)} %add_rsqrt_fusion), kind=kOutput, calls=%fused_computation.17 | convolution fusion | flops 8431861760 | bytes 72261632 | tf_op jit(solution)/shard_map/dot_general | solution.py:22
  77.0 13.8 %fusion.48 = (f32[2048]{0:T(1024)S(1)}, bf16[2048,640]{0,1:T(8,128)(2,1)S(1)}) fusion(bf16[2048,3200]{1,0:T(8,128)(2,1)} %get-tuple-element.24, bf16[2,3200,640]{2,1,0:T(8,128)(2,1)} %param.15, bf16[1,2048,640]{1,2,0:T(8,128)(2,1)S(1)} %copy.20), kind=kOutput, calls=%fused_computation.79 | convolution fusion | flops 8395159552 | bytes 22454272 | tf_op jit(solution)/shard_map/dot_general | solution.py:10
  90.8 0.0 copy-start.5
  90.8 0.0 copy-start.8
  90.8 17.3 %fusion.52 = f32[2048,3200]{1,0:T(8,128)} fusion(bf16[2,640,3200]{2,1,0:T(8,128)(2,1)} %param.14, bf16[2048,640]{0,1:T(8,128)(2,1)S(1)} %get-tuple-element.27, f32[2048]{0:T(1024)S(1)} %fusion.103), kind=kOutput, calls=%fused_computation.83 | convolution fusion | flops 8392540160 | bytes 32940032 | tf_op jit(solution)/shard_map/jvp()/dot_general | solution.py:22
  108.1 0.0 copy-done.8
  108.1 34.5 %fusion.2 = (bf16[2048,3200]{1,0:T(8,128)(2,1)}, f32[2048,3200]{1,0:T(8,128)}) fusion(f32[2048,3200]{1,0:T(8,128)} %fusion.52, bf16[2048,3200]{1,0:T(8,128)(2,1)} %convolution_convert_fusion.1, bf16[2,640,3200]{2,1,0:T(8,128)(2,1)} %param.13, bf16[2048,640]{0,1:T(8,128)(2,1)S(1)} %get-tuple-element.27, f32[2048]{0:T(1024)S(1)} %fusion.103), kind=kOutput, calls=%fused_computation.8 | convolution fusion | flops 8471183360 | bytes 85368832 | tf_op jit(solution)/shard_map/jvp()/dot_general | solution.py:21
  142.5 18.2 %fusion.82 = bf16[2048,640]{0,1:T(8,128)(2,1)} fusion(bf16[2,640,3200]{2,1,0:T(8,128)(2,1)} %param.14, bf16[2048,3200]{1,0:T(8,128)(2,1)} %convolution_convert_fusion.1, f32[2048,3200]{1,0:T(8,128)} %get-tuple-element.29), kind=kOutput, calls=%fused_computation.109 | convolution fusion | flops 8429240320 | bytes 46039040 | tf_op jit(solution)/shard_map/transpose(jvp())/dot_general | solution.py:22
  160.7 23.0 %fusion.39 = bf16[1,3200,640]{2,1,0:T(8,128)(2,1)} fusion(f32[2048,3200]{1,0:T(8,128)} %fusion.52, bf16[1,2048,640]{2,1,0:T(8,128)(2,1)} %param.12, f32[2048,3200]{1,0:T(8,128)} %get-tuple-element.29), kind=kOutput, calls=%fused_computation.70 | convolution fusion | flops 8429977600 | bytes 59146240 | tf_op jit(solution)/shard_map/transpose(jvp())/dot_general | solution.py:10
  183.7 0.0 copy-done.6
  183.7 14.2 %fusion.50 = (f32[2048]{0:T(1024)S(1)}, bf16[2048,640]{0,1:T(8,128)(2,1)S(1)}) fusion(bf16[2048,640]{0,1:T(8,128)(2,1)S(1)} %copy-done.6, bf16[2048,640]{0,1:T(8,128)(2,1)} %fusion.82, bf16[2048,3200]{1,0:T(8,128)(2,1)} %get-tuple-element.28, bf16[2,640,3200]{2,1,0:T(8,128)(2,1)} %param.13), kind=kOutput, calls=%fused_computation.81 | convolution fusion | flops 8395159552 | bytes 25075712 | tf_op jit(solution)/shard_map/transpose(jvp())/dot_general | solution.py:21
  197.9 0.0 slice-start
  197.9 1.8 fusion.92
  199.7 0.0 slice-start.1
  199.8 15.4 %fusion.41 = bf16[1,3200,640]{2,1,0:T(8,128)(2,1)} fusion(bf16[2048,3200]{1,0:T(8,128)(2,1)} %get-tuple-element.24, bf16[2048,640]{0,1:T(8,128)(2,1)S(1)} %fusion.92), kind=kOutput, calls=%fused_computation.72 | convolution fusion | flops 8390656000 | bytes 19824640 | tf_op jit(solution)/shard_map/transpose(jvp())/dot_general | solution.py:10
  215.2 0.0 slice-done
  215.2 13.4 %convolution_convert_fusion = bf16[2048,3200]{1,0:T(8,128)(2,1)} fusion(bf16[2048,640]{0,1:T(8,128)(2,1)S(1)} %fusion.92, bf16[2,3200,640]{2,1,0:T(8,128)(2,1)S(1)} %bitcast.81), kind=kOutput, calls=%fused_computation.49 | convolution fusion | flops 8395161600 | bytes 19824640 | tf_op jit(solution)/shard_map/transpose(jvp())/dot_general | solution.py:10
  228.6 18.8 %fusion.43 = bf16[1,640,3200]{2,1,0:T(8,128)(2,1)} fusion(bf16[2048,3200]{1,0:T(8,128)(2,1)} %convolution_convert_fusion.1, bf16[2048,640]{0,1:T(8,128)(2,1)S(1)} %copy-done.6, f32[2048]{0:T(1024)S(1)} %fusion.103, f32[2048,3200]{1,0:T(8,128)} %get-tuple-element.29), kind=kOutput, calls=%fused_computation.74 | convolution fusion | flops 8433909760 | bytes 46047232 | tf_op jit(solution)/shard_map/transpose(jvp())/dot_general | solution.py:22
  247.4 15.7 %fusion.40 = bf16[1,640,3200]{2,1,0:T(8,128)(2,1)} fusion(bf16[2048,3200]{1,0:T(8,128)(2,1)} %get-tuple-element.28, bf16[2048,640]{0,1:T(8,128)(2,1)} %copy-done.5, f32[2048]{0:T(1024)S(1)} %fusion.103), kind=kOutput, calls=%fused_computation.71 | convolution fusion | flops 8392540160 | bytes 19832832 | tf_op jit(solution)/shard_map/transpose(jvp())/dot_general | solution.py:21
  263.1 19.1 %fusion.42 = bf16[1,640,3200]{2,1,0:T(8,128)(2,1)} fusion(bf16[2048,3200]{1,0:T(8,128)(2,1)} %convolution_convert_fusion, f32[2048,3200]{1,0:T(8,128)} %fusion.65, bf16[1,2048,640]{1,2,0:T(8,128)(2,1)S(1)} %copy-done.2, f32[2048]{0:T(1024)S(1)} %copy-done.11), kind=kOutput, calls=%fused_computation.73 | convolution fusion | flops 8433909760 | bytes 46047232 | tf_op jit(solution)/shard_map/transpose(jvp())/dot_general | solution.py:22
  282.2 27.3 %fusion.36 = bf16[1,640,3200]{2,1,0:T(8,128)(2,1)} fusion(f32[2048,3200]{1,0:T(8,128)} %fusion.65, f32[2048,3200]{1,0:T(8,128)} %get-tuple-element.25, bf16[2048,3200]{1,0:T(8,128)(2,1)} %convolution_convert_fusion, bf16[1,2048,640]{1,2,0:T(8,128)(2,1)S(1)} %copy-done.2, f32[2048]{0:T(1024)S(1)} %copy-done.11), kind=kOutput, calls=%fused_computation.69 | convolution fusion | flops 8466677760 | bytes 72261632 | tf_op jit(solution)/shard_map/transpose(jvp())/dot_general | solution.py:21
  309.4 0.1 all-reduce.3.cloned.1.call-update
  309.5 192.7 %all-reduce.3.cloned.1.call-done = (bf16[1,640,3200]{2,1,0:T(8,128)(2,1)}, bf16[1,640,3200]{2,1,0:T(8,128)(2,1)}, bf16[1,640,3200]{2,1,0:T(8,128)(2,1)}, bf16[1,...) async-done(((bf16[1,640,3200]{2,1,0:T(8,128)(2,1)}, bf16[1,640,3200]{2,1,0:T(8,128)(2,1)}, bf16[1,640,3200]{2,1,0:T(8,128)(2,1)}, ...) | async-done | bytes 24576016 | tf_op jit(solution)/shard_map/psum | solution.py:45
  502.2 30.3 %fusion.23 = (bf16[2,3200,640]{2,1,0:T(8,128)(2,1)}, f32[2,3200,640]{2,1,0:T(8,128)}, f32[2,3200,640]{2,1,0:T(8,128)}) fusion(bf16[2,3200,640]{2,1,0:T(8,128)(2,1)} %param.15, bf16[1,3200,640]{2,1,0:T(8,128)(2,1)} %get-tuple-element.13, bf16[1,3200,640]{2,1,0:T(8,128)(2,1)} %get-tuple-element.14, f32[2,3200,640]{2,1,0:T(8,128)} %param.21, ...), kind=kLoop, calls=%fused_computation.44 | loop fusion | flops 77824000 | bytes 90112000 | tf_op jit(solution)/shard_map/convert_element_type | solution.py:30
  532.5 54.5 %fusion.15 = (bf16[2,640,3200]{2,1,0:T(8,128)(2,1)}, f32[2,640,3200]{2,1,0:T(8,128)}, f32[2,640,3200]{2,1,0:T(8,128)}, bf16[2,640,3200]{2,1,0:T(8,128)(2,1)}, f3...) fusion(bf16[2,640,3200]{2,1,0:T(8,128)(2,1)} %param.13, bf16[1,640,3200]{2,1,0:T(8,128)(2,1)S(1)} %copy-done.3, ...), kind=kLoop, calls=%fused_computation.36 | loop fusion | flops 155648000 | bytes 180224000 | tf_op jit(solution)/shard_map/convert_element_type | solution.py:30
  (24 shorter events, 0.1 us)
Async XLA Ops:
  7.2 495.0 %all-reduce.3.cloned.1.call-start = ((), (), s32[]{:S(2)}) async-start(), calls=%async_computation | async-start | bytes 49152000 | tf_op jit(solution)/shard_map/psum | solution.py:45
  10.3 66.7 %copy-start.1 = (bf16[1,2048,640]{1,2,0:T(8,128)(2,1)}, bf16[1,2048,640]{1,2,0:T(8,128)(2,1)S(1)}, u32[]{:S(2)}) copy-start(bf16[1,2048,640]{1,2,0:T(8,128)(2,1)S(1)} %copy.20) | copy-start | bytes 7864324
  10.9 37.9 %copy-start.10 = (f32[2048]{0:T(1024)}, f32[2048]{0:T(1024)S(1)}, u32[]{:S(2)}) copy-start(f32[2048]{0:T(1024)S(1)} %add_rsqrt_fusion) | copy-start | bytes 24580
  15.6 16.4 %copy-start.7 = (bf16[1,2048,640]{2,1,0:T(8,128)(2,1)S(1)}, bf16[1,2048,640]{2,1,0:T(8,128)(2,1)}, u32[]{:S(2)}) copy-start(bf16[1,2048,640]{2,1,0:T(8,128)(2,1)} %param.11) | copy-start | bytes 7864324
  90.8 17.3 %copy-start.5 = (bf16[2048,640]{0,1:T(8,128)(2,1)}, bf16[2048,640]{0,1:T(8,128)(2,1)S(1)}, u32[]{:S(2)}) copy-start(bf16[2048,640]{0,1:T(8,128)(2,1)S(1)} %get-tuple-element.27) | copy-start | bytes 7864324
  90.8 17.3 %copy-start.8 = (f32[2048]{0:T(1024)}, f32[2048]{0:T(1024)S(1)}, u32[]{:S(2)}) copy-start(f32[2048]{0:T(1024)S(1)} %get-tuple-element.26) | copy-start | bytes 24580
  160.7 23.0 %copy-start.6 = (bf16[2048,640]{0,1:T(8,128)(2,1)S(1)}, bf16[2048,640]{0,1:T(8,128)(2,1)}, u32[]{:S(2)}) copy-start(bf16[2048,640]{0,1:T(8,128)(2,1)} %copy-done.5) | copy-start | bytes 7864324
  183.7 14.2 %copy-start.9 = (f32[2048]{0:T(1024)S(1)}, f32[2048]{0:T(1024)}, u32[]{:S(2)}) copy-start(f32[2048]{0:T(1024)} %copy-done.8) | copy-start | bytes 24580
  183.7 14.2 %copy-start = (bf16[1,2048,640]{1,2,0:T(8,128)(2,1)S(1)}, bf16[1,2048,640]{1,2,0:T(8,128)(2,1)}, u32[]{:S(2)}) copy-start(bf16[1,2048,640]{1,2,0:T(8,128)(2,1)} %copy.21) | copy-start | bytes 7864324
  197.9 17.3 %slice-start = ((s8[8192000]{0:T(1024)(128)(4,1)}), s8[4194304]{0:T(1024)(128)(4,1)S(1)}, s32[]{:S(2)}) async-start(s8[8192000]{0:T(1024)(128)(4,1)} %bitcast.80), calls=%async_computation.1 | async-start | bytes 8388608
  199.7 15.4 %slice-start.1 = ((s8[8192000]{0:T(1024)(128)(4,1)}), s8[3997696]{0:T(1024)(128)(4,1)S(1)}, s32[]{:S(2)}) async-start(s8[8192000]{0:T(1024)(128)(4,1)} %bitcast.80), calls=%async_computation.2 | async-start | bytes 7995392
  247.4 15.7 %copy-start.2 = (bf16[1,2048,640]{1,2,0:T(8,128)(2,1)S(1)}, bf16[1,2048,640]{1,2,0:T(8,128)(2,1)}, u32[]{:S(2)}) copy-start(bf16[1,2048,640]{1,2,0:T(8,128)(2,1)} %copy-done.1) | copy-start | bytes 7864324
  247.4 15.7 %copy-start.11 = (f32[2048]{0:T(1024)S(1)}, f32[2048]{0:T(1024)}, u32[]{:S(2)}) copy-start(f32[2048]{0:T(1024)} %copy-done.10) | copy-start | bytes 24580
  502.2 30.3 %copy-start.3 = (bf16[1,640,3200]{2,1,0:T(8,128)(2,1)S(1)}, bf16[1,640,3200]{2,1,0:T(8,128)(2,1)}, u32[]{:S(2)}) copy-start(bf16[1,640,3200]{2,1,0:T(8,128)(2,1)} %get-tuple-element.9) | copy-start | bytes 12288004
  502.2 30.3 %copy-start.4 = (bf16[1,640,3200]{2,1,0:T(8,128)(2,1)S(1)}, bf16[1,640,3200]{2,1,0:T(8,128)(2,1)}, u32[]{:S(2)}) copy-start(bf16[1,640,3200]{2,1,0:T(8,128)(2,1)} %get-tuple-element.10) | copy-start | bytes 12288004
Sparse Core Ops, SparseCore 0:
  309.6 192.5 all-reduce.2
where the time goes:
time: 603 us; the launch traced here: 594 us
  matrix products  292 us (48%)
  waiting for transfers between devices  193 us (32%)
  other arithmetic  87.1 us (14%)
  between operations  14.7 us (2%)
  local copies, waits for them, and re-layouts  7.8 us (1%)
    psum x1, waiting for transfers between devices, step(): summed[number] = [lax.psum(by_w[name], 'dp') for name in NAMES]  193 us
    dot_general x5, matrix products, layer(): gate = jnp.dot(a, w['w_gate'], preferred_element_type=jnp.float32)  108 us
    dot_general x5, matrix products, layer(): up = jnp.dot(a, w['w_up'], preferred_element_type=jnp.float32)  102 us
    convert_element_type x2, other arithmetic, adamw(): return ((w - 0.02 * step).astype(jnp.bfloat16), m, v)  84.8 us
    dot_general x5, matrix products, matmul(): jnp.dot(a, w, preferred_element_type=jnp.float32).astype(jnp.bfloat16)  82 us
  transfers between devices with their start and end apart: 1, of which 1 were waited for; matrix products, arithmetic and copies ran while one was open for 0% of the time, Pallas kernels for 0%

commit v1 on v0

v1 whole, which is shorter than its diff:
```python
import functools
import math

import jax
import jax.numpy as jnp
from jax import lax
from jax.experimental import pallas as pl
from jax.experimental.pallas import tpu as pltpu
from jax.sharding import PartitionSpec as P

BF16, F32 = jnp.bfloat16, jnp.float32
TILE = 256
LANES = 128
ROWS = 512
VMEM_LIMIT = 60 * 1024 * 1024


def dot(a, b, contract=((1,), (0,))):
    return lax.dot_general(a, b, (contract, ((), ())), preferred_element_type=F32)


def dot_t(a, b):
    return dot(a, b, ((1,), (1,)))


def scale_of(wide):
    return lax.rsqrt(jnp.mean(wide * wide, -1, keepdims=True) + 1e-6)


def sigmoid(x):
    return 0.5 * jnp.tanh(0.5 * x) + 0.5


def params(limit=VMEM_LIMIT):
    return pltpu.CompilerParams(vmem_limit_bytes=limit)


def whole(shape, layer=None):
    if layer is None:
        return pl.BlockSpec(shape, lambda *_: (0,) * len(shape), pipeline_mode=pl.Buffered(1))
    return pl.BlockSpec((None, *shape), lambda *_: (layer,) + (0,) * len(shape), pipeline_mode=pl.Buffered(1))


def cuts(total, size):
    return [(at, min(size, total - at)) for at in range(0, total, size)]


def forward_kernel(h_ref, dy_ref, wg_ref, wu_ref, wd_ref, gate_ref, up_ref, at_ref, h1_ref, a1_ref, a1t_ref, dyt_ref, hid_ref):
    h = h_ref[...].astype(F32)
    a = (h * scale_of(h)).astype(BF16)
    at_ref[...] = a.T
    dyt_ref[...] = dy_ref[...].T
    for at, n in cuts(wg_ref.shape[1], 1280):
        gate = dot(a, wg_ref[:, at : at + n])
        up = dot(a, wu_ref[:, at : at + n])
        gate_ref[:, at : at + n] = gate
        up_ref[:, at : at + n] = up
        hid_ref[:, at : at + n] = (gate * sigmoid(gate) * up).astype(BF16)
    z = dot(hid_ref[...], wd_ref[...]).astype(BF16)
    h1 = (h + z.astype(F32)).astype(BF16)
    h1_ref[...] = h1
    h1 = h1.astype(F32)
    a1 = (h1 * scale_of(h1)).astype(BF16)
    a1_ref[...] = a1
    a1t_ref[...] = a1.T


def forward(h, dy, wg, wu, wd, layer):
    t, d = h.shape
    f = wg.shape[2]
    rows = pl.BlockSpec((ROWS, d), lambda i: (i, 0))
    hidden = pl.BlockSpec((ROWS, f), lambda i: (i, 0))
    columns = pl.BlockSpec((d, ROWS), lambda i: (0, i))
    return pl.pallas_call(
        forward_kernel,
        grid=(t // ROWS,),
        in_specs=[rows, rows, whole((d, f), layer), whole((d, f), layer), whole((f, d), layer)],
        out_specs=[hidden, hidden, columns, rows, rows, columns, columns],
        out_shape=[
            jax.ShapeDtypeStruct((t, f), F32),
            jax.ShapeDtypeStruct((t, f), F32),
            jax.ShapeDtypeStruct((d, t), BF16),
            jax.ShapeDtypeStruct((t, d), BF16),
            jax.ShapeDtypeStruct((t, d), BF16),
            jax.ShapeDtypeStruct((d, t), BF16),
            jax.ShapeDtypeStruct((d, t), BF16),
        ],
        scratch_shapes=[pltpu.VMEM((ROWS, f), BF16)],
        compiler_params=params(),
        cost_estimate=pl.CostEstimate(flops=6 * t * d * f, bytes_accessed=8 * t * f, transcendentals=t * f),
        name="forward",
    )(h, dy, wg, wu, wd)


def hidden_gradients(gate, up, dhid):
    dhid = dhid.astype(BF16).astype(F32)
    s = sigmoid(gate)
    silu = gate * s
    hid = (silu * up).astype(BF16)
    dup = (dhid * silu).astype(BF16)
    dgate = (dhid * up * (s + silu * (1.0 - s))).astype(BF16)
    return hid, dgate, dup


def store_gradients(g_ref, at_ref, dyt_ref, hid_ref, dgate_ref, dup_ref):
    d = at_ref.shape[0]
    for i, (left, right) in enumerate(((at_ref, dgate_ref), (at_ref, dup_ref), (dyt_ref, hid_ref))):
        g = dot(left[...], right[...]).astype(BF16)
        for k in range(TILE // LANES):
            g_ref[(3 * k + i) * d : (3 * k + i + 1) * d, :] = g[:, k * LANES : (k + 1) * LANES]


def last_kernel(a_ref, at_ref, dy_ref, dyt_ref, wg_ref, wu_ref, wd_ref, g_ref, dgate_ref, dup_ref, hid_ref):
    for at, n in cuts(a_ref.shape[0], ROWS):
        here = slice(at, at + n)
        gate = dot(a_ref[here, :], wg_ref[...])
        up = dot(a_ref[here, :], wu_ref[...])
        dhid = dot_t(dy_ref[here, :], wd_ref[...])
        hid_ref[here, :], dgate_ref[here, :], dup_ref[here, :] = hidden_gradients(gate, up, dhid)
    store_gradients(g_ref, at_ref, dyt_ref, hid_ref, dgate_ref, dup_ref)


def flat(d, rows):
    return pl.BlockSpec((3 * d * (TILE // LANES), LANES), lambda j: (j, 0)), jax.ShapeDtypeStruct((rows, LANES), BF16)


def last_backward(a, at, dy, dyt, wg, wu, wd, layer, rows):
    t, d = a.shape
    f = wg.shape[2]
    columns = pl.BlockSpec((None, d, TILE), lambda j: (layer, 0, j))
    out = pl.BlockSpec((t, TILE), lambda j: (0, j))
    spec, shape = flat(d, rows)
    return pl.pallas_call(
        last_kernel,
        grid=(pl.cdiv(f, TILE),),
        in_specs=[
            whole((t, d)),
            whole((d, t)),
            whole((t, d)),
            whole((d, t)),
            columns,
            columns,
            pl.BlockSpec((None, TILE, d), lambda j: (layer, j, 0)),
        ],
        out_specs=[spec, out, out],
        out_shape=[shape, jax.ShapeDtypeStruct((t, f), BF16), jax.ShapeDtypeStruct((t, f), BF16)],
        scratch_shapes=[pltpu.VMEM((t, TILE), BF16)],
        compiler_params=params(),
        cost_estimate=pl.CostEstimate(flops=12 * t * d * f, bytes_accessed=6 * t * f, transcendentals=t * f),
        name="last_backward",
    )(a, at, dy, dyt, wg, wu, wd)


def first_kernel(gate_ref, up_ref, at_ref, dy_ref, dyt_ref, wd_ref, g_ref, hid_ref, dgate_ref, dup_ref):
    for at, n in cuts(dy_ref.shape[0], ROWS):
        here = slice(at, at + n)
        dhid = dot_t(dy_ref[here, :], wd_ref[...])
        hid_ref[here, :], dgate_ref[here, :], dup_ref[here, :] = hidden_gradients(gate_ref[here, :], up_ref[here, :], dhid)
    store_gradients(g_ref, at_ref, dyt_ref, hid_ref, dgate_ref, dup_ref)


def first_backward(gate, up, at, dy, dyt, wd, layer, rows):
    t, d = dy.shape
    f = wd.shape[1]
    hidden = pl.BlockSpec((t, TILE), lambda j: (0, j))
    spec, shape = flat(d, rows)
    return pl.pallas_call(
        first_kernel,
        grid=(pl.cdiv(f, TILE),),
        in_specs=[hidden, hidden, whole((d, t)), whole((t, d)), whole((d, t)), pl.BlockSpec((None, TILE, d), lambda j: (layer, j, 0))],
        out_specs=spec,
        out_shape=shape,
        scratch_shapes=[pltpu.VMEM((t, TILE), BF16)] * 3,
        compiler_params=params(),
        cost_estimate=pl.CostEstimate(flops=8 * t * d * f, bytes_accessed=8 * t * f, transcendentals=t * f),
        name="first_backward",
    )(gate, up, at, dy, dyt, wd)


def input_kernel(h_ref, dy_ref, wg_ref, wu_ref, dgate_ref, dup_ref, dh_ref, dht_ref):
    da = dot_t(dgate_ref[...], wg_ref[...]) + dot_t(dup_ref[...], wu_ref[...])
    da = da.astype(BF16).astype(F32)
    h = h_ref[...].astype(F32)
    scale = scale_of(h)
    along = jnp.sum(da * h, -1, keepdims=True)
    by_norm = da * scale - h * (scale * scale * scale * along / h.shape[1])
    dh = (dy_ref[...].astype(F32) + by_norm.astype(BF16).astype(F32)).astype(BF16)
    dh_ref[...] = dh
    dht_ref[...] = dh.T


def input_gradient(h, dy, wg, wu, dgate, dup, layer):
    t, d = h.shape
    f = wg.shape[2]
    rows = pl.BlockSpec((ROWS, d), lambda i: (i, 0))
    hidden = pl.BlockSpec((ROWS, f), lambda i: (i, 0))
    return pl.pallas_call(
        input_kernel,
        grid=(t // ROWS,),
        in_specs=[rows, rows, whole((d, f), layer), whole((d, f), layer), hidden, hidden],
        out_specs=[rows, pl.BlockSpec((d, ROWS), lambda i: (0, i))],
        out_shape=[jax.ShapeDtypeStruct((t, d), BF16), jax.ShapeDtypeStruct((d, t), BF16)],
        compiler_params=params(),
        cost_estimate=pl.CostEstimate(flops=4 * t * d * f, bytes_accessed=4 * t * f, transcendentals=0),
        name="input_gradient",
    )(h, dy, wg, wu, dgate, dup)


def where(side):
    me = lax.axis_index("dp")
    core = me % 2
    return core, me // 2 // side, me // 2 % side


def device(side, core, x, y, k, w):
    u, v = x * (1 - core) + y * core, y * (1 - core) + x * core
    u, v = (u + k) % side, (v + w) % side
    return ((u * (1 - core) + v * core) * side + v * (1 - core) + u * core) * 2 + core


def add_into(out, rows, *refs):
    step = next(n for n in (64, 32, 16) if rows % n == 0)

    def body(i, _):
        here = pl.ds(pl.multiple_of(i * step, step), step)
        total = refs[0][here, :].astype(F32)
        for ref in refs[1:]:
            total = total + ref[here, :].astype(F32)
        out[here, :] = total.astype(out.dtype)
        return _

    lax.fori_loop(0, rows // step, body, 0)


def scatter_kernel(side, g_ref, out_ref, mine, theirs, relay, beside, stay, relay2, beside2, load_sem, pair_send, pair_recv, send, recv):
    core, x, y = where(side)
    n = out_ref.shape[0]
    half = n // 2
    partner = (x * side + y) * 2 + 1 - core
    right, left = device(side, core, x, y, 1, 0), device(side, core, x, y, side - 1, 0)
    ahead, behind = device(side, core, x, y, 0, 1), device(side, core, x, y, 0, side - 1)

    barrier = pltpu.get_barrier_semaphore()
    for other in (partner, right, left, ahead, behind):
        pl.semaphore_signal(barrier, inc=1, device_id={"dp": other}, device_id_type=pl.DeviceIdType.MESH)
    pl.semaphore_wait(barrier, 5)

    def remote(src, dst, send_sem, recv_sem, to):
        return pltpu.make_async_remote_copy(
            src_ref=src, dst_ref=dst, send_sem=send_sem, recv_sem=recv_sem, device_id={"dp": to}, device_id_type=pl.DeviceIdType.MESH
        )

    def segment(of, k, w):
        row = device(side, of, x, y, k, w) * n
        return g_ref.at[pl.ds(pl.multiple_of(row, n), n), :]

    def slot(k, w):
        return pl.ds((k * side + w) * n, n)

    order = [(k, w) for k in (2, 1, 3, 0) for w in range(side)]
    pair, load = {}, {}
    for k, w in order:
        i = k * side + w
        pair[k, w] = remote(segment(1 - core, k, w), theirs.at[slot(k, w), :], pair_send.at[i], pair_recv.at[i], partner)
        pair[k, w].start()
        load[k, w] = pltpu.make_async_copy(segment(core, k, w), mine.at[slot(k, w), :], load_sem.at[i])
        load[k, w].start()

    def here(k, w):
        load[k, w].wait()
        pair[k, w].wait_recv()

    def two(ref, k, w):
        return ref.at[pl.ds((k * side + w) * n, 2 * n), :]

    copies = []

    def go(i, src, dst, to):
        copies.append(remote(src, dst, send.at[i], recv.at[i], to))
        copies[-1].start()
        return copies[-1]

    def summed(k, w):
        for one in (w, w + 1):
            here(k, one)
        add_into(two(mine, k, w), 2 * n, two(mine, k, w), two(theirs, k, w))

    summed(2, 0)
    from_left = go(0, two(mine, 2, 0), relay.at[pl.ds(0, 2 * n), :], right)
    summed(2, 2)
    from_right = go(1, two(mine, 2, 2), relay.at[pl.ds(2 * n, 2 * n), :], left)
    summed(1, 2)
    by_left = [go(2, two(mine, 1, 2), two(beside, 0, 2), right)]
    summed(3, 0)
    by_right = [go(3, two(mine, 3, 0), two(beside, 1, 0), left)]
    for one in (0, 1):
        here(1, one)
    from_left.wait_recv()
    add_into(two(mine, 1, 0), 2 * n, two(mine, 1, 0), two(theirs, 1, 0), relay.at[pl.ds(0, 2 * n), :])
    by_left.append(go(4, two(mine, 1, 0), two(beside, 0, 0), right))
    for one in (2, 3):
        here(3, one)
    from_right.wait_recv()
    add_into(two(mine, 3, 2), 2 * n, two(mine, 3, 2), two(theirs, 3, 2), relay.at[pl.ds(2 * n, 2 * n), :])
    by_right.append(go(5, two(mine, 3, 2), two(beside, 1, 2), left))
    for one in range(side):
        here(0, one)
    for one in by_left + by_right:
        one.wait_recv()

    def own(w, out):
        at = slot(0, w)
        add_into(out, n, mine.at[at, :], theirs.at[at, :], beside.at[slot(0, w), :], beside.at[slot(1, w), :])

    def part(w, which):
        return mine.at[pl.ds(w * n + which * half, half), :]

    own(2, mine.at[slot(0, 2), :])
    from_left = go(6, part(2, 0), relay2.at[pl.ds(0, half), :], ahead)
    from_right = go(7, part(2, 1), relay2.at[pl.ds(half, half), :], behind)
    own(1, mine.at[slot(0, 1), :])
    by_left = [go(8, part(1, 1), beside2.at[pl.ds(half, half), :], ahead)]
    own(3, mine.at[slot(0, 3), :])
    by_right = [go(9, part(3, 0), beside2.at[pl.ds(n, half), :], behind)]
    from_left.wait_recv()
    add_into(part(1, 0), half, part(1, 0), relay2.at[pl.ds(0, half), :])
    by_left.append(go(10, part(1, 0), beside2.at[pl.ds(0, half), :], ahead))
    from_right.wait_recv()
    add_into(part(3, 1), half, part(3, 1), relay2.at[pl.ds(half, half), :])
    by_right.append(go(11, part(3, 1), beside2.at[pl.ds(n + half, half), :], behind))
    own(0, stay)
    for one in by_left + by_right:
        one.wait_recv()
    add_into(out_ref, n, stay, beside2.at[pl.ds(0, n), :], beside2.at[pl.ds(n, n), :])
    for one in list(pair.values()) + copies:
        one.wait_send()


def scatter(g, side, collective_id):
    n = g.shape[0] // (2 * side * side)
    return pl.pallas_call(
        functools.partial(scatter_kernel, side),
        in_specs=[pl.BlockSpec(memory_space=pl.ANY)],
        out_specs=pl.BlockSpec(memory_space=pltpu.VMEM),
        out_shape=jax.ShapeDtypeStruct((n, LANES), BF16),
        scratch_shapes=[
            pltpu.VMEM((side * side * n, LANES), BF16),
            pltpu.VMEM((side * side * n, LANES), BF16),
            pltpu.VMEM((side * n, LANES), BF16),
            pltpu.VMEM((2 * side * n, LANES), BF16),
            pltpu.VMEM((n, LANES), F32),
            pltpu.VMEM((n, LANES), BF16),
            pltpu.VMEM((2 * n, LANES), BF16),
            pltpu.SemaphoreType.DMA((side * side,)),
            pltpu.SemaphoreType.DMA((side * side,)),
            pltpu.SemaphoreType.DMA((side * side,)),
            pltpu.SemaphoreType.DMA((12,)),
            pltpu.SemaphoreType.DMA((12,)),
        ],
        compiler_params=pltpu.CompilerParams(collective_id=collective_id, has_side_effects=True, vmem_limit_bytes=VMEM_LIMIT),
        cost_estimate=pl.CostEstimate(flops=40_000_000_000, bytes_accessed=2 * g.size, transcendentals=0),
        name="scatter",
    )(g)


def adamw(w, m, v, g):
    m = 0.9 * m + 0.1 * g
    v = 0.95 * v + 0.05 * g * g
    step = m * lax.rsqrt(v + 1e-8) + 0.1 * w
    return (w - 0.02 * step).astype(BF16), m, v


def adamw_kernel(given, g_ref, *refs):
    ins, outs = refs[:9], refs[9 + given :]
    d = g_ref.shape[0] // 3
    for i in range(3):
        g = g_ref[i * d : (i + 1) * d, :]
        g = (g.T if i == 2 else g).astype(F32)
        outs[i][...], outs[3 + i][...], outs[6 + i][...] = adamw(ins[i][...].astype(F32), ins[3 + i][...], ins[6 + i][...], g)


def update(g, arrays, so_far, layer):
    _, d, f = arrays[0].shape
    wide = pl.BlockSpec((None, d, LANES), lambda j: (layer, 0, j))
    tall = pl.BlockSpec((None, LANES, d), lambda j: (layer, j, 0))
    specs = [wide, wide, tall] * 3
    given = 0 if so_far is None else 9
    return pl.pallas_call(
        functools.partial(adamw_kernel, given),
        grid=(f // LANES,),
        in_specs=[pl.BlockSpec((3 * d, LANES), lambda j: (j, 0))] + specs + [pl.BlockSpec(memory_space=pl.ANY)] * given,
        out_specs=specs,
        out_shape=[jax.ShapeDtypeStruct(one.shape, one.dtype) for one in arrays],
        input_output_aliases={10 + i: i for i in range(given)},
        compiler_params=params(),
        cost_estimate=pl.CostEstimate(flops=36 * d * f, bytes_accessed=66 * d * f, transcendentals=3 * d * f),
        name="adamw",
    )(g, *arrays, *(so_far or ()))


def solution(mesh):
    size = mesh.shape["dp"]
    side = math.isqrt(size // 2)

    def step(x, dy, *arrays):
        wg, wu, wd = arrays[:3]
        layers, d, f = wg.shape
        assert layers == 2 and side == 4 and 2 * side * side == size and f % LANES == 0
        dy = dy[0]
        rows = pl.cdiv(3 * d * f // LANES, 32 * size) * 32 * size
        gate, up, at0, h1, a1, a1t, dyt = forward(x[0], dy, wg, wu, wd, 0)
        g, dgate, dup = last_backward(a1, a1t, dy, dyt, wg, wu, wd, 1, rows)
        late = lax.psum(g, "dp")
        dh, dht = input_gradient(h1, dy, wg, wu, dgate, dup, 1)
        g = first_backward(gate, up, at0, dh, dht, wd, 0, rows)
        early = scatter(g, side, 0)
        late, early = lax.optimization_barrier((late, early))
        early = lax.all_gather(early, "dp", axis=0, tiled=True)
        new = update(late, arrays, None, 1)
        return tuple(update(early, arrays, new, 0))

    return jax.shard_map(
        step,
        mesh=mesh,
        in_specs=(P(("rep", "dp"), None, None),) * 2 + (P(None, None, None),) * 9,
        out_specs=(P("rep", None, None),) * 9,
        check_vma=False,
    )
```

time: 603 us -> 384 us (0.64); the launches traced: 594 us -> 383 us
  Pallas kernels: 0 us -> 362 us
  matrix products: 292 us -> 0 us
  waiting for transfers between devices: 193 us -> 6.91 us
  other arithmetic: 87.1 us -> 0 us
  local copies, waits for them, and re-layouts: 7.8 us -> 0 us
    pallas_call x0 -> x7, Pallas kernels: none -> 362 us  [the longest x2 101 us: update(): pl.pallas_call(functools.partial(adamw_kernel, given), grid=(f // LANES,)...]
    dot_general x15 -> x0, matrix products: 292 us -> none  [the longest x5 108 us: layer(): gate = jnp.dot(a, w['w_gate'], preferred_element_type=jnp.float32)]
    psum x1, waiting for transfers between devices: 193 us -> 0.02 us  [step(): late = lax.psum(g, 'dp')]
    convert_element_type x2 -> x0, other arithmetic: 84.8 us -> none  [adamw(): return ((w - 0.02 * step).astype(jnp.bfloat16), m, v)]
    unnamed x30 -> x0, local copies, waits for them, and re-layouts: 7.8 us -> none
    all_gather x0 -> x1, waiting for transfers between devices: none -> 6.78 us  [step(): early = lax.all_gather(early, 'dp', axis=0, tiled=True)]
  transfers between devices with their start and end apart: 1 -> 2, of which waited for: 1 -> 1; matrix products, arithmetic and copies ran while one was open for 0% -> 0% of each run, Pallas kernels for 0% -> 53%
where the time goes in v1:
time: 384 us; the launch traced here: 383 us
  Pallas kernels  362 us (94%)
  between operations  14.1 us (4%)
  waiting for transfers between devices  6.91 us (2%)
    pallas_call x2, Pallas kernels, update(): pl.pallas_call(functools.partial(adamw_kernel, given), grid=(f // LANES,)...  101 us
    pallas_call x1, Pallas kernels, scatter(): pl.pallas_call(functools.partial(scatter_kernel, side), in_specs=[pl.Bloc...  72.8 us
    pallas_call x1, Pallas kernels, last_backward(): pl.pallas_call(last_kernel, grid=(pl.cdiv(f, TILE),), in_specs=[whole((t,...  67.3 us
    pallas_call x1, Pallas kernels, first_backward(): pl.pallas_call(first_kernel, grid=(pl.cdiv(f, TILE),), in_specs=[hidden,...  47.3 us
    pallas_call x1, Pallas kernels, forward(): pl.pallas_call(forward_kernel, grid=(t // ROWS,), in_specs=[rows, rows, w...  42.7 us
    pallas_call x1, Pallas kernels, input_gradient(): pl.pallas_call(input_kernel, grid=(t // ROWS,), in_specs=[rows, rows, who...  30.4 us
  transfers between devices with their start and end apart: 2, of which 1 were waited for; matrix products, arithmetic and copies ran while one was open for 0% of the time, Pallas kernels for 53%

profile of v1, /device:TPU:97, one launch (start us, length us, event | category | flops | bytes accessed | tf_op | source)
XLA Modules:
  0.0 383.4 jit_solution(12449264646797323615)
XLA Ops:
  7.2 0.1 all-reduce.2.cloned.1.call-start
  7.3 42.7 %forward.1 = (f32[2048,3200]{1,0:T(8,128)}, f32[2048,3200]{1,0:T(8,128)}, bf16[640,2048]{1,0:T(8,128)(2,1)}, bf16[2048,640]{1,0:T(8,128)(2,1)}, bf16[2048,640]{1...) custom-call(bf16[2048,640]{1,0:T(8,128)(2,1)} %bitcast.2, bf16[2048,640]{1,0:T(8,128)(2,1)} %bitcast.3, ...), custom_call_target="tpu_custom_call" | custom-call | flops 25165824000 | bytes 52428800 | tf_op jit(solution)/shard_map/forward/pallas_call | solution.py:74
  49.9 67.3 %last_backward.1 = (bf16[48128,128]{1,0:T(8,128)(2,1)}, bf16[2048,3200]{1,0:T(8,128)(2,1)}, bf16[2048,3200]{1,0:T(8,128)(2,1)}) custom-call(bf16[2048,640]{1,0:T(8,128)(2,1)} %get-tuple-element.32.a_ref, bf16[640,2048]{1,0:T(8,128)(2,1)} %get-tuple-element.33.at_ref, bf16[2048,640]{1,0:T(8,128)(2,1)} %bitcast.4, ...), custom_call_target="tpu_custom_call" | custom-call | flops 50331648000 | bytes 39321600 | tf_op jit(solution)/shard_map/last_backward/pallas_call | solution.py:133
  117.2 0.1 all-reduce.2.cloned.1.call-update
  117.3 0.2 all-gather.2.cloned.1.call-start
  117.6 30.4 %input_gradient.1 = (bf16[2048,640]{1,0:T(8,128)(2,1)}, bf16[640,2048]{1,0:T(8,128)(2,1)}) custom-call(bf16[2048,640]{1,0:T(8,128)(2,1)} %get-tuple-element.39.h_ref, bf16[2048,640]{1,0:T(8,128)(2,1)} %bitcast.5, bf16[2,640,3200]{2,1,0:T(8,128)(2,1)} %refs_0_.3, bf16[2,640,3200]{2,1,0:T(8,128)(2,1)} %refs_1_.3, ...), custom_call_target="tpu_custom_call" | custom-call | flops 16777216000 | bytes 26214400 | tf_op jit(solution)/shard_map/input_gradient/pallas_call | solution.py:197
  148.0 47.3 %first_backward.1.g_ref = bf16[48128,128]{1,0:T(8,128)(2,1)} custom-call(f32[2048,3200]{1,0:T(8,128)} %get-tuple-element.36.gate_ref, f32[2048,3200]{1,0:T(8,128)} %get-tuple-element.37.up_ref, bf16[640,2048]{1,0:T(8,128)(2,1)} %get-tuple-element.38.at_ref, bf16[2048,640]{1,0:T(8,128)(2,1)} %get-tuple-element.42.dy_ref, ...), custom_call_target="tpu_custom_call" | custom-call | flops 33554432000 | bytes 52428800 | tf_op jit(solution)/shard_map/first_backward/pallas_call | solution.py:167
  195.3 72.8 %scatter.1 = bf16[1504,128]{1,0:T(8,128)(2,1)} custom-call(bf16[48128,128]{1,0:T(8,128)(2,1)} %first_backward.1.g_ref), custom_call_target="tpu_custom_call" | custom-call | flops 40000000000 | bytes 12320768 | tf_op jit(solution)/shard_map/scatter/pallas_call | solution.py:341
  268.2 0.0 all-reduce.2.cloned.1.call-done.g_ref
  268.2 0.1 all-gather.2.cloned.1.call-update
  268.3 51.0 %adamw.2 = (bf16[2,640,3200]{2,1,0:T(8,128)(2,1)}, bf16[2,640,3200]{2,1,0:T(8,128)(2,1)}, bf16[2,3200,640]{2,1,0:T(8,128)(2,1)}, f32[2,640,3200]{2,1,0:T(8,128)}...) custom-call(bf16[48128,128]{1,0:T(8,128)(2,1)} %all-reduce.2.cloned., ...), custom_call_target="tpu_custom_call" | custom-call | flops 73728000 | bytes 135168000 | tf_op jit(solution)/shard_map/adamw/pallas_call | solution.py:388
  319.3 6.8 %all-gather.2.cloned.1.call-done.g_ref = bf16[48128,128]{1,0:T(8,128)(2,1)} async-done(((bf16[1504,128]{1,0:T(8,128)(2,1)}), bf16[48128,128]{1,0:T(8,128)(2,1)}) %all-gather.2.cloned.1.call-update) | async-done | bytes 12320784 | tf_op jit(solution)/shard_map/all_gather | solution.py:418
  326.0 50.4 %adamw.3 = (bf16[2,640,3200]{2,1,0:T(8,128)(2,1)}, bf16[2,640,3200]{2,1,0:T(8,128)(2,1)}, bf16[2,3200,640]{2,1,0:T(8,128)(2,1)}, f32[2,640,3200]{2,1,0:T(8,128)}...) custom-call(bf16[48128,128]{1,0:T(8,128)(2,1)} %all-gather.2.cloned., ...), custom_call_target="tpu_custom_call", output_to_operand_aliasing={{0}: (10, {}), {1}: (11, {}), {2}: (12, {}), {3}: (13, {}),... | custom-call | flops 73728000 | bytes 135168000 | tf_op jit(solution)/shard_map/adamw/pallas_call | solution.py:388
Async XLA Ops:
  7.2 261.0 %all-reduce.2.cloned.1.call-start = ((), (), s32[]{:S(2)}) async-start(), calls=%async_computation | async-start | bytes 24641536 | tf_op jit(solution)/shard_map/psum | solution.py:413
  117.3 208.7 %all-gather.2.cloned.1.call-start = ((), (), s32[]{:S(2)}) async-start(), calls=%async_computation.1 | async-start | bytes 12705792 | tf_op jit(solution)/shard_map/all_gather | solution.py:418
Sparse Core Ops, SparseCore 0:
  117.4 150.1 all-reduce.1
  269.7 56.3 all-gather.1
